TPU v7x, 32 devices: a whole 2x2x4 slice. The times are simulated.
32 devices in a mesh: member: 1, span: 32 (over z, y, x, core).
Axes of the slice: x: 2, y: 2, z: 4, core: 2. Of those that a mesh axis runs over, the one named last changes fastest.
Arguments:
- field: float32 [1024, 23040], P(('member', 'span')), may hold values from -60 to 60
- day_table: int32 [1024], P('member'), may hold values from 0 to 364
- band_owner: int32 [32], P('member'), may hold values from 0 to 31, as said below
- sea_mask: int32 [23040], replicated, may hold values 0 or 1
Outputs:
- coeff_out: float32 [13, 23040], P(None, ('member', 'span'))
- variance_out: float32 [23040], P(('member', 'span'))
Inputs may be any that keep to these rules, and one draw needn't show every extreme that they name: `band_owner`: a permutation of 0 to 31.
All inputs are finite; a program needn't handle non-finite values.
Results may differ from a plain program's by a relative error of at most 0.00013.
Values sent between devices are 32-bit elements; how exact they have to be, the bound alone decides.
No kernel may reach another device: no remote copies, remote signals or barrier semaphores. Data moves between devices by JAX's collectives and lax.ppermute only.
A program may use at most 64 MiB of HBM per device.

v0:
```python
import math

import jax
import jax.numpy as jnp
from jax import lax
from jax.sharding import PartitionSpec as P

HARMS = 6


def harmonic_basis(day_values):
    angles = day_values.astype(jnp.float32) * (2.0 * math.pi / 365.0)
    basis_rows = [jnp.ones_like(angles)]
    for order in range(1, HARMS + 1):
        basis_rows.append(jnp.cos(order * angles))
        basis_rows.append(jnp.sin(order * angles))
    return jnp.stack(basis_rows, 0)


def on_device(field, day_table, band_owner, sea_mask):
    groups = lax.axis_size("span")
    own_index = lax.axis_index("span")
    steps_dev, cells = field.shape
    band_cells = cells // groups
    design = harmonic_basis(day_table)
    total_steps = design.shape[1]
    gram_matrix = jnp.dot(design, design.T, precision=lax.Precision.HIGHEST)
    factor = jnp.linalg.cholesky(gram_matrix)
    slots = jnp.arange(groups, dtype=jnp.int32)
    own_band = jnp.sum(jnp.where(band_owner == own_index, slots, 0))
    source_band = jnp.sum(
        jnp.where(band_owner[None, :] == slots[:, None], slots[None, :], 0), axis=1
    )
    blocks = field.reshape(steps_dev, groups, band_cells)
    outgoing = jnp.take(blocks, source_band, axis=1).reshape(steps_dev, cells)
    weight_mask = lax.dynamic_slice_in_dim(sea_mask, own_band * band_cells, band_cells).astype(
        jnp.float32
    )
    series = lax.all_to_all(outgoing, "span", split_axis=1, concat_axis=0, tiled=True)
    projection = jnp.dot(design, series, precision=lax.Precision.HIGHEST)
    coeffs = jax.scipy.linalg.cho_solve((factor, True), projection)
    residual = series - jnp.dot(design.T, coeffs, precision=lax.Precision.HIGHEST)
    variance = jnp.sum(residual * residual, axis=0) / total_steps
    coeffs = coeffs * weight_mask[None, :]
    variance = variance * weight_mask
    return (coeffs, variance)


def solution(mesh):
    in_specs = (P(("member", "span"), None), P("member"), P("member"), P())
    out_specs = (P(None, ("member", "span")), P(("member", "span")))
    return jax.shard_map(
        on_device, mesh=mesh, in_specs=in_specs, out_specs=out_specs, check_vma=False
    )
```

profile of v0, /device:TPU:0, one launch (start us, length us, event | category | flops | bytes accessed | tf_op | source)
XLA Modules:
  0.0 103.2 jit_solution(3279304344381537644)
XLA Ops:
  0.6 0.8 select_reduce_fusion
  1.4 4.1 %reshape.51 = f32[32,32,720]{2,1,0:T(8,128)S(1)} reshape(f32[32,23040]{1,0:T(8,128)} %param.4) | data formatting | bytes 5898240 | tf_op jit(solution)/shard_map/reshape | solution.py:34
  5.6 3.5 %copy.13 = f32[32,32,720]{2,0,1:T(8,128)} copy(f32[32,32,720]{2,1,0:T(8,128)S(1)} %reshape.51) | data formatting | bytes 5898240 | tf_op jit(solution)/shard_map/reshape | solution.py:34
  9.1 2.6 %gather_fusion = f32[32,32,720]{2,1,0:T(8,128)S(1)} fusion(f32[32,32,720]{2,0,1:T(8,128)} %copy.13, s32[1024]{0:T(1024)S(1)} %pad_clamp_fusion), kind=kCustom, calls=%fused_computation | custom fusion | bytes 5898368 | tf_op jit(solution)/shard_map/jit(_take)/gather | solution.py:35
  11.7 2.0 %select_bitcast_fusion = f32[32,32,720]{2,0,1:T(8,128)} fusion(f32[32,32,720]{2,1,0:T(8,128)S(1)} %gather_fusion, pred[32]{0:T(512)(128)(4,1)S(1)} %compare_and_fusion), kind=kLoop, calls=%fused_computation.1 | loop fusion | flops 737280 | bytes 5898272 | tf_op jit(solution)/shard_map/jit(_take)/select_n | solution.py:35
  13.8 0.0 copy-start
  13.8 0.0 copy-start.1
  13.8 7.3 %all-to-all-start = ((f32[32,32,720]{2,0,1:T(8,128)}), f32[32,32,720]{2,0,1:T(8,128)S(1)}, u32[]{:S(2)}, u32[]{:S(2)}) async-start(f32[32,32,720]{2,0,1:T(8,128)} %select_bitcast_fusion), calls=%async_computation | async-start | bytes 6291456 | tf_op jit(solution)/shard_map/all_to_all | solution.py:39
  21.1 0.0 copy-done
  21.1 0.1 fusion.16
  21.2 0.1 stack.51
  21.3 0.2 fusion.20
  21.5 0.1 copy.12
  21.6 1.2 %cholesky.16 = f32[13,13]{1,0:T(8,128)S(1)} custom-call(f32[13,13]{1,0:T(8,128)S(1)} %fusion.5), custom_call_target="Cholesky" | custom-call | tf_op jit(solution)/shard_map/jit(cholesky)/cholesky | solution.py:28
  22.9 0.6 compare_reduce_fusion
  23.5 0.6 fusion
  24.2 1.0 custom-call.10
  25.2 0.0 copy-done.1
  25.2 0.6 fusion.18
  26.5 66.0 %all-to-all-done = f32[32,32,720]{2,0,1:T(8,128)S(1)} async-done(((f32[32,32,720]{2,0,1:T(8,128)}), f32[32,32,720]{2,0,1:T(8,128)S(1)}, u32[]{:S(2)}, u32[]{:S(2)}) %all-to-all-start) | async-done | bytes 2949152 | tf_op jit(solution)/shard_map/all_to_all | solution.py:39
  92.4 1.6 %fusion.21 = f32[13,720]{1,0:T(8,128)S(1)} fusion(f32[13,1024]{1,0:T(8,128)S(1)} %stack.51, f32[1024,720]{1,0:T(8,128)S(1)} %bitcast.40), kind=kOutput, calls=%fused_computation.46 | convolution fusion | flops 115015680 | bytes 3039808 | tf_op jit(solution)/shard_map/dot_general | solution.py:40
  94.0 2.3 %copy.14 = f32[1024,720]{0,1:T(8,128)} copy(f32[1024,720]{1,0:T(8,128)S(1)} %bitcast.41) | data formatting | bytes 5898240 | tf_op jit(solution)/shard_map/all_to_all | solution.py:39
  96.3 0.2 fusion.3
  96.6 0.2 fusion.1
  96.7 4.5 %multiply_reduce_fusion = f32[720]{0:T(1024)S(1)} fusion(f32[1024,720]{0,1:T(8,128)} %copy.14, f32[13,1024]{1,0:T(8,128)S(1)} %stack.51, f32[13,720]{1,0:T(8,128)S(1)} %fusion.1), kind=kOutput, calls=%fused_computation.2 | convolution fusion | flops 117226800 | bytes 3042688 | tf_op jit(solution)/shard_map/dot_general | solution.py:42
  101.2 1.4 %multiply_multiply_fusion = (f32[720]{0:T(1024)}, f32[720]{0:T(1024)S(1)}) fusion(f32[720]{0:T(1024)S(1)} %multiply_reduce_fusion, s32[23040]{0:T(1024)} %param.7, s32[]{:T(128)S(6)} %select_n.43), kind=kLoop, calls=%fused_computation.18 | loop fusion | flops 2160 | bytes 11524 | tf_op jit(solution)/shard_map/mul | solution.py:45
  102.6 0.6 broadcast_multiply_fusion
  (6 shorter events, 0.1 us)
Async XLA Ops:
  13.8 7.3 %copy-start = (s32[1024]{0:T(1024)S(1)}, s32[1024]{0:T(1024)}, u32[]{:S(2)}) copy-start(s32[1024]{0:T(1024)} %param.5) | copy-start | bytes 12292
  13.8 11.4 %copy-start.1 = (s32[32]{0:T(128)S(1)}, s32[32]{0:T(128)}, u32[]{:S(2)}) copy-start(s32[32]{0:T(128)} %param.6) | copy-start | bytes 388
  13.8 78.7 %all-to-all-start = ((f32[32,32,720]{2,0,1:T(8,128)}), f32[32,32,720]{2,0,1:T(8,128)S(1)}, u32[]{:S(2)}, u32[]{:S(2)}) async-start(f32[32,32,720]{2,0,1:T(8,128)} %select_bitcast_fusion), calls=%async_computation | async-start | bytes 6291456 | tf_op jit(solution)/shard_map/all_to_all | solution.py:39
where the time goes:
time: 104 us; the launch traced here: 103 us
  waiting for transfers between devices  66 us (63%)
  local copies, waits for them, and re-layouts  12.8 us (12%)
  other arithmetic  9.1 us (9%)
  starting transfers between devices  7.33 us (7%)
  matrix products  6.68 us (6%)
  between operations  1.39 us (1%)
    all_to_all x1, waiting for transfers between devices, on_device(): lax.all_to_all(outgoing, 'span', split_axis=1, concat_axis=0, tiled=True)  66 us
    reshape x2, local copies, waits for them, and re-layouts, on_device(): blocks = field.reshape(steps_dev, groups, band_cells)  7.63 us
    all_to_all x1, starting transfers between devices, on_device(): lax.all_to_all(outgoing, 'span', split_axis=1, concat_axis=0, tiled=True)  7.33 us
    dot_general x1, matrix products, on_device(): jnp.dot(design.T, coeffs, precision=lax.Precision.HIGHEST)  4.5 us
    gather x1, local copies, waits for them, and re-layouts, on_device(): outgoing = jnp.take(blocks, source_band, axis=1).reshape(steps_dev, cells)  2.64 us
    all_to_all x1, local copies, waits for them, and re-layouts, on_device(): lax.all_to_all(outgoing, 'span', split_axis=1, concat_axis=0, tiled=True)  2.3 us
  transfers between devices with their start and end apart: 1, of which 1 were waited for; matrix products, arithmetic and copies ran while one was open for 5% of the time, Pallas kernels for 0%

commit v1 on v0

v1 whole, which is shorter than its diff:
```python
import functools
import math

import jax
import jax.numpy as jnp
from jax import lax
from jax.experimental import pallas as pl
from jax.experimental.pallas import tpu as pltpu
from jax.sharding import PartitionSpec as P

HARMS = 6
LANES = 128
ROWS = 16


def harmonic_basis(day_values):
    angles = day_values.astype(jnp.float32) * (2.0 * math.pi / 365.0)
    basis_rows = [jnp.ones_like(angles)]
    for order in range(1, HARMS + 1):
        basis_rows.append(jnp.cos(order * angles))
        basis_rows.append(jnp.sin(order * angles))
    return jnp.stack(basis_rows, 0)


def split_radices(groups):
    radices = []
    rest = groups
    if rest % 2 == 0:
        radices.append(2)
        rest //= 2
    while rest % 4 == 0:
        radices.append(4)
        rest //= 4
    if rest > 1 or not radices:
        radices.append(rest)
    return radices


def round_up(value, unit):
    return -(-value // unit) * unit


def chunk_of(cells, most):
    tiles = cells // LANES
    best = max(t for t in range(1, tiles + 1) if tiles % t == 0 and t * LANES <= most)
    return best * LANES


def rounded(x):
    return lax.reduce_precision(x, 8, 7)


def split_design(design, steps_dev):
    d = jnp.pad(design, ((0, ROWS - design.shape[0]), (0, 0)))
    high = rounded(d)
    mid = rounded(d - high)
    low = rounded(d - high - mid)
    none = jnp.zeros_like(d)
    stacked = jnp.concatenate(
        [
            jnp.concatenate([high, high, high], 1),
            jnp.concatenate([mid, mid, none], 1),
            jnp.concatenate([low, none, none], 1),
        ],
        0,
    )
    return stacked.astype(jnp.bfloat16)


def sums_kernel(order_ref, lhs_ref, field_ref, *refs, cols, band, width, chunk, lead):
    outs, scratch = refs[:-1], refs[-1]
    step = pl.program_id(0)
    f = field_ref[...]
    high = f.astype(jnp.bfloat16)
    left = f - high.astype(jnp.float32)
    mid = left.astype(jnp.bfloat16)
    low = (left - mid.astype(jnp.float32)).astype(jnp.bfloat16)
    stacked = jnp.concatenate([high, mid, low], 0)
    parts = jnp.dot(lhs_ref[...], stacked, preferred_element_type=jnp.float32)
    total = parts[:ROWS] + (parts[ROWS : 2 * ROWS] + parts[2 * ROWS :])
    squares = jnp.sum(f * f, axis=0, keepdims=True)
    row = lax.broadcasted_iota(jnp.int32, total.shape, 0)
    scratch[:, pl.ds(pl.multiple_of(step * chunk, LANES), chunk)] = jnp.where(
        row == cols, squares, total
    )

    @pl.when(step == pl.num_programs(0) - 1)
    def _():
        edge = scratch.shape[1] - 2 * LANES
        scratch[:, edge:] = jnp.zeros((ROWS, 2 * LANES), jnp.float32)
        for q in range(lead * len(outs)):
            start = order_ref[q] * band
            offset = lax.rem(start, LANES)
            base = pl.multiple_of(start - offset, LANES)
            window = scratch[:, pl.ds(base, width + LANES)]
            span = width + LANES
            rolled = pltpu.roll(window, lax.rem(span - offset, span), 1)
            outs[q // lead][q % lead] = rolled[:, :width]


def fit_kernel(inv_ref, invt_ref, mask_ref, *refs, cols, band, steps):
    parts, coeff_ref, var_ref = refs[:-2], refs[-2], refs[-1]
    total = parts[0][0]
    for part in parts[1:]:
        total = total + part[0]
    hp = lax.Precision.HIGHEST
    half = jnp.dot(inv_ref[...], total, precision=hp, preferred_element_type=jnp.float32)
    coeffs = jnp.dot(invt_ref[...], half, precision=hp, preferred_element_type=jnp.float32)
    squares = total[cols : cols + 1]
    rest = squares - jnp.sum(half * half, axis=0, keepdims=True)
    variance = jnp.maximum(rest, 0.0) / steps
    mask = mask_ref[...]
    coeff_ref[...] = coeffs[:cols, :band] * mask
    var_ref[...] = variance[:, :band] * mask


def on_device(field, day_table, band_owner, sea_mask):
    groups = lax.axis_size("span")
    own_index = lax.axis_index("span")
    steps_dev, cells = field.shape
    band = cells // groups
    width = round_up(band, LANES)
    steps = day_table.shape[0]
    radices = split_radices(groups)
    strides = [math.prod(radices[:r]) for r in range(len(radices))]

    slots = jnp.arange(groups, dtype=jnp.int32)
    target = jnp.zeros_like(slots)
    inner = groups
    for radix, stride in zip(radices, strides):
        inner //= radix
        target = target + ((slots // inner + own_index // stride) % radix) * stride
    order = jnp.sum(
        jnp.where(band_owner[None, :] == target[:, None], slots[None, :], 0), axis=1
    )
    days = lax.dynamic_slice_in_dim(day_table, own_index * steps_dev, steps_dev)
    own_design = harmonic_basis(days)
    cols = own_design.shape[0]
    lhs = split_design(own_design, steps_dev)

    lead = groups // radices[0]
    chunk = chunk_of(cells, 4608)
    pieces = pl.pallas_call(
        functools.partial(
            sums_kernel, cols=cols, band=band, width=width, chunk=chunk, lead=lead
        ),
        grid_spec=pltpu.PrefetchScalarGridSpec(
            num_scalar_prefetch=1,
            grid=(cells // chunk,),
            in_specs=[
                pl.BlockSpec(lhs.shape, lambda s, o: (0, 0)),
                pl.BlockSpec((steps_dev, chunk), lambda s, o: (0, s)),
            ],
            out_specs=[pl.BlockSpec((lead, ROWS, width), lambda s, o: (0, 0, 0))] * radices[0],
            scratch_shapes=[pltpu.VMEM((ROWS, cells + 2 * LANES), jnp.float32)],
        ),
        out_shape=[jax.ShapeDtypeStruct((lead, ROWS, width), jnp.float32)] * radices[0],
        name="sums",
    )(order, lhs, field)

    design = harmonic_basis(day_table)
    gram = jnp.dot(design, design.T, precision=lax.Precision.HIGHEST)
    factor = jnp.linalg.cholesky(gram)
    inverse = lax.linalg.triangular_solve(
        factor, jnp.eye(cols, dtype=jnp.float32), left_side=True, lower=True
    )
    inverse = jnp.pad(inverse, ((0, ROWS - cols), (0, ROWS - cols)))
    own_band = jnp.sum(jnp.where(band_owner == own_index, slots, 0))
    mask = lax.dynamic_slice_in_dim(sea_mask, own_band * band, band).astype(jnp.float32)

    pieces = list(pieces)
    for r, (radix, stride) in enumerate(zip(radices, strides)):
        received = []
        for shift in range(1, radix):
            pairs = []
            for source in range(groups):
                digit = source // stride % radix
                pairs.append((source, source + ((digit + shift) % radix - digit) * stride))
            received.append(lax.ppermute(pieces[shift], "span", pairs))
        pieces = [pieces[0]] + received
        if r + 1 < len(radices):
            total = functools.reduce(jnp.add, pieces)
            part = total.shape[0] // radices[r + 1]
            pieces = [total[k * part : (k + 1) * part] for k in range(radices[r + 1])]

    coeffs, variance = pl.pallas_call(
        functools.partial(fit_kernel, cols=cols, band=band, steps=steps),
        out_shape=[
            jax.ShapeDtypeStruct((cols, band), jnp.float32),
            jax.ShapeDtypeStruct((1, band), jnp.float32),
        ],
        name="fit",
    )(inverse, inverse.T, mask[None, :], *pieces)
    return (coeffs, variance.reshape(band))


def solution(mesh):
    in_specs = (P(("member", "span"), None), P("member"), P("member"), P())
    out_specs = (P(None, ("member", "span")), P(("member", "span")))
    return jax.shard_map(
        on_device, mesh=mesh, in_specs=in_specs, out_specs=out_specs, check_vma=False
    )
```

time: 104 us -> 43.3 us (0.42)
  waiting for transfers between devices: 66 us -> 7.01 us
  local copies, waits for them, and re-layouts: 12.8 us -> 3.46 us
  Pallas kernels: 0 us -> 8.54 us
  matrix products: 6.68 us -> 0.37 us
  starting transfers between devices: 7.33 us -> 11.5 us
  other arithmetic: 9.1 us -> 10.6 us
    all_to_all x1 -> x0, waiting for transfers between devices: 66 us -> none  [on_device(): lax.all_to_all(outgoing, 'span', split_axis=1, concat_axis=0, tiled=True)]
    ppermute x0 -> x7, starting transfers between devices: none -> 11.5 us  [on_device(): received.append(lax.ppermute(pieces[shift], 'span', pairs))]
    pallas_call x0 -> x2, Pallas kernels: none -> 8.54 us  [the longest x1 6.62 us: on_device(): pl.pallas_call(functools.partial(sums_kernel, cols=cols, band=band, width...]
    reshape x2 -> x0, local copies, waits for them, and re-layouts: 7.63 us -> none  [on_device(): blocks = field.reshape(steps_dev, groups, band_cells)]
    all_to_all x1 -> x0, starting transfers between devices: 7.33 us -> none  [on_device(): lax.all_to_all(outgoing, 'span', split_axis=1, concat_axis=0, tiled=True)]
    ppermute x0 -> x7, waiting for transfers between devices: none -> 7.01 us  [on_device(): received.append(lax.ppermute(pieces[shift], 'span', pairs))]
    dot_general x3 -> x1, matrix products: 6.25 us -> 0.17 us  [on_device(): gram = jnp.dot(design, design.T, precision=lax.Precision.HIGHEST)]
    gather x1 -> x0, local copies, waits for them, and re-layouts: 2.64 us -> none  [on_device(): outgoing = jnp.take(blocks, source_band, axis=1).reshape(steps_dev, cells)]
  transfers between devices with their start and end apart: 1 -> 7, of which waited for: 1 -> 5; matrix products, arithmetic and copies ran while one was open for 5% -> 17% of each run, Pallas kernels for 0% -> 0%
where the time goes in v1:
time: 43.3 us; the launch traced here: 42.9 us
  starting transfers between devices  11.5 us (27%)
  other arithmetic  10.6 us (24%)
  Pallas kernels  8.54 us (20%)
  waiting for transfers between devices  7.01 us (16%)
  local copies, waits for them, and re-layouts  3.46 us (8%)
  between operations  1.4 us (3%)
    ppermute x7, starting transfers between devices, on_device(): received.append(lax.ppermute(pieces[shift], 'span', pairs))  11.5 us
    ppermute x7, waiting for transfers between devices, on_device(): received.append(lax.ppermute(pieces[shift], 'span', pairs))  7.01 us
    pallas_call x1, Pallas kernels, on_device(): pl.pallas_call(functools.partial(sums_kernel, cols=cols, band=band, width...  6.62 us
    pallas_call x1, Pallas kernels, on_device(): pl.pallas_call(functools.partial(fit_kernel, cols=cols, band=band, steps=...  1.91 us
    another operation x3, other arithmetic, on_device(): factor = jnp.linalg.cholesky(gram)  1.87 us
    another operation x2, other arithmetic, on_device(): lax.linalg.triangular_solve(factor, jnp.eye(cols, dtype=jnp.float32), lef...  1.65 us
    reduce_sum x1, other arithmetic, on_device(): jnp.sum(jnp.where(band_owner[None, :] == target[:, None], slots[None, :],...  1.35 us
    pallas_call x1, other arithmetic, on_device(): pl.pallas_call(functools.partial(fit_kernel, cols=cols, band=band, steps=...  1.28 us
  transfers between devices with their start and end apart: 7, of which 5 were waited for; matrix products, arithmetic and copies ran while one was open for 17% of the time, Pallas kernels for 0%

profile of v1, /device:TPU:0, one launch (start us, length us, event | category | flops | bytes accessed | tf_op | source)
XLA Modules:
  0.0 42.9 jit_solution(14822394697947072184)
XLA Ops:
  0.6 0.9 %sine_bitcast_fusion = (f32[1,32]{1,0:T(1,128)S(1)}, s32[32]{0:T(128)S(1)}) fusion(s32[1024]{0:T(1024)} %param.5, s32[]{:T(128)S(6)} %select_n.82), kind=kLoop, calls=%fused_computation.69 | loop fusion | flops 64 | bytes 388 | tf_op jit(solution)/shard_map/stack | solution.py:22
  1.7 1.4 %select_reduce_fusion.order_ref = s32[32]{0:T(128)} fusion(s32[32]{0:T(128)} %param.6, s32[32]{0:T(128)S(1)} %fusion.23), kind=kLoop, calls=%fused_computation.5 | loop fusion | flops 3040 | bytes 384 | tf_op jit(solution)/shard_map/reduce_sum | solution.py:133
  3.1 0.7 %fusion.3.lhs_ref = bf16[48,96]{1,0:T(8,128)(2,1)} fusion(bf16[16,32]{1,0:T(8,128)(2,1)S(1)} %get-tuple-element.20, bf16[16,32]{1,0:T(8,128)(2,1)S(1)} %broadcast_in_dim.31, bf16[16,32]{1,0:T(8,128)(2,1)S(1)} %get-tuple-element.21, bf16[16,32]{1,0:T(8,128)(2,1)S(1)} %get-tuple-element.19), kind=kLoop, calls=%fused_computation.6 | loop fusion | flops 73728 | bytes 13312 | tf_op jit(solution)/shard_map/concatenate | solution.py:59
  3.8 6.6 %sums.1 = (f32[16,16,768]{2,1,0:T(8,128)}, f32[16,16,768]{2,1,0:T(8,128)}) custom-call(s32[32]{0:T(128)} %select_reduce_fusion.order_ref, bf16[48,96]{1,0:T(8,128)(2,1)} %fusion.3.lhs_ref, f32[32,23040]{1,0:T(8,128)} %field_ref.1), custom_call_target="tpu_custom_call" | custom-call | tf_op jit(solution)/shard_map/sums/pallas_call | solution.py:143
  10.4 0.5 %collective-permute-start = (f32[16,16,768]{2,1,0:T(8,128)}, f32[16,16,768]{2,1,0:T(8,128)S(1)}, u32[]{:S(2)}, u32[]{:S(2)}) collective-permute-start(f32[16,16,768]{2,1,0:T(8,128)} %get-tuple-element.7), channel_id=1, source_target_pairs={{0,1},{1,0},{2,3},{3,2},{4,5},{5,4},{6,7},{7,6},{8,9},{9,8},{10,11... | collective-permute-start | bytes 2359304 | tf_op jit(solution)/shard_map/ppermute | solution.py:179
  11.4 1.2 %cholesky.17 = f32[13,13]{1,0:T(8,128)S(1)} custom-call(f32[13,13]{1,0:T(8,128)S(1)} %fusion.9), custom_call_target="Cholesky" | custom-call | tf_op jit(solution)/shard_map/jit(cholesky)/cholesky | solution.py:163
  12.6 0.6 %compare_reduce_fusion = pred[]{:T(512)} fusion(f32[13]{0:T(128)S(1)} %select_reduce_fusion.1), kind=kLoop, calls=%fused_computation.53 | loop fusion | flops 25 | bytes 53 | tf_op jit(solution)/shard_map/jit(cholesky)/cholesky | solution.py:163
  13.3 0.6 %fusion.4 = f32[1,13,13]{2,1,0:T(8,128)S(1)} fusion(f32[13,13]{1,0:T(8,128)S(1)} %cholesky.17, pred[]{:T(512)} %compare_reduce_fusion), kind=kLoop, calls=%fused_computation.12 | loop fusion | flops 676 | bytes 1353 | tf_op jit(solution)/shard_map/triangular_solve | solution.py:164
  13.9 1.0 %custom-call.6 = f32[1,13,13]{1,2,0:T(8,128)S(1)} custom-call(f32[1,13,13]{2,1,0:T(8,128)S(1)} %fusion.4), custom_call_target="InvertDiagBlocksLowerTriangular" | custom-call | tf_op jit(solution)/shard_map/triangular_solve | solution.py:164
  14.9 0.2 fusion.7
  15.1 1.2 %add.131 = f32[16,16,768]{2,1,0:T(8,128)S(1)} add(f32[16,16,768]{2,1,0:T(8,128)} %get-tuple-element.6, f32[16,16,768]{2,1,0:T(8,128)S(1)} %collective-permute-done) | non-fusion elementwise | flops 196608 | bytes 2359296 | tf_op jit(solution)/shard_map/add | solution.py:182
  16.4 2.5 %collective-permute-start.1 = (f32[4,16,768]{2,1,0:T(8,128)S(1)}, f32[4,16,768]{2,1,0:T(8,128)S(1)}, u32[]{:S(2)}, u32[]{:S(2)}) collective-permute-start(f32[4,16,768]{2,1,0:T(8,128)S(1)} %get-tuple-element.12), channel_id=1, source_target_pairs={{0,2},{1,3},{2,4},{3,5},{4,6},{5,7},{6,0},{7,1},{8,10},{9,11},{10,... | collective-permute-start | bytes 589832 | tf_op jit(solution)/shard_map/ppermute | solution.py:179
  19.0 1.5 %collective-permute-start.2 = (f32[4,16,768]{2,1,0:T(8,128)S(1)}, f32[4,16,768]{2,1,0:T(8,128)S(1)}, u32[]{:S(2)}, u32[]{:S(2)}) collective-permute-start(f32[4,16,768]{2,1,0:T(8,128)S(1)} %get-tuple-element.14), channel_id=1, source_target_pairs={{0,4},{1,5},{2,6},{3,7},{4,0},{5,1},{6,2},{7,3},{8,12},{9,13},{10,... | collective-permute-start | bytes 589832 | tf_op jit(solution)/shard_map/ppermute | solution.py:179
  20.5 1.4 %collective-permute-start.3 = (f32[4,16,768]{2,1,0:T(8,128)S(1)}, f32[4,16,768]{2,1,0:T(8,128)S(1)}, u32[]{:S(2)}, u32[]{:S(2)}) collective-permute-start(f32[4,16,768]{2,1,0:T(8,128)S(1)} %get-tuple-element.13), channel_id=1, source_target_pairs={{0,6},{1,7},{2,0},{3,1},{4,2},{5,3},{6,4},{7,5},{8,14},{9,15},{10,... | collective-permute-start | bytes 589832 | tf_op jit(solution)/shard_map/ppermute | solution.py:179
  21.9 0.6 %fusion.26 = s32[]{:T(128)} fusion(s32[32]{0:T(128)S(1)} %copy-done.4, s32[]{:T(128)S(6)} %axis_index.12), kind=kLoop, calls=%fused_computation.63 | loop fusion | flops 95 | bytes 136 | tf_op jit(solution)/shard_map/reduce_sum | solution.py:168
  23.2 0.6 %pad_bitcast_fusion.invt_ref = f32[16,16]{1,0:T(8,128)} fusion(f32[13,13]{0,1:T(8,128)S(1)} %fusion.7), kind=kLoop, calls=%fused_computation.87 | loop fusion | bytes 1700 | tf_op jit(solution)/shard_map/transpose | solution.py:193
  23.8 1.9 %collective-permute-done.1 = f32[4,16,768]{2,1,0:T(8,128)S(1)} collective-permute-done((f32[4,16,768]{2,1,0:T(8,128)S(1)}, f32[4,16,768]{2,1,0:T(8,128)S(1)}, u32[]{:S(2)}, u32[]{:S(2)}) %collective-permute-start.1) | collective-permute-done | bytes 196640 | tf_op jit(solution)/shard_map/ppermute | solution.py:179
  25.7 4.0 %collective-permute-done.2 = f32[4,16,768]{2,1,0:T(8,128)S(1)} collective-permute-done((f32[4,16,768]{2,1,0:T(8,128)S(1)}, f32[4,16,768]{2,1,0:T(8,128)S(1)}, u32[]{:S(2)}, u32[]{:S(2)}) %collective-permute-start.2) | collective-permute-done | bytes 196640 | tf_op jit(solution)/shard_map/ppermute | solution.py:179
  29.7 0.3 collective-permute-done.3
  30.0 0.6 %fusion.33 = (f32[1,16,768]{2,1,0:T(8,128)S(1)}, f32[1,16,768]{2,1,0:T(8,128)S(1)}, f32[1,16,768]{2,1,0:T(8,128)S(1)}, f32[1,16,768]{2,1,0:T(8,128)}) fusion(f32[4,16,768]{2,1,0:T(8,128)S(1)} %fusion.1), kind=kLoop, calls=%fused_computation.89 | loop fusion | bytes 393216 | tf_op jit(solution)/shard_map/slice | solution.py:184
  30.7 1.6 %collective-permute-start.4 = (f32[1,16,768]{2,1,0:T(8,128)S(1)}, f32[1,16,768]{2,1,0:T(8,128)S(1)}, u32[]{:S(2)}, u32[]{:S(2)}) collective-permute-start(f32[1,16,768]{2,1,0:T(8,128)S(1)} %get-tuple-element.17), channel_id=1, source_target_pairs={{0,8},{1,9},{2,10},{3,11},{4,12},{5,13},{6,14},{7,15},{8,16},{9,17... | collective-permute-start | bytes 147464 | tf_op jit(solution)/shard_map/ppermute | solution.py:179
  32.2 2.6 %collective-permute-start.5 = (f32[1,16,768]{2,1,0:T(8,128)S(1)}, f32[1,16,768]{2,1,0:T(8,128)S(1)}, u32[]{:S(2)}, u32[]{:S(2)}) collective-permute-start(f32[1,16,768]{2,1,0:T(8,128)S(1)} %get-tuple-element.16), channel_id=1, source_target_pairs={{0,16},{1,17},{2,18},{3,19},{4,20},{5,21},{6,22},{7,23},{8,24},{9,... | collective-permute-start | bytes 147464 | tf_op jit(solution)/shard_map/ppermute | solution.py:179
  34.8 1.3 %collective-permute-start.6 = (f32[1,16,768]{2,1,0:T(8,128)S(1)}, f32[1,16,768]{2,1,0:T(8,128)S(1)}, u32[]{:S(2)}, u32[]{:S(2)}) collective-permute-start(f32[1,16,768]{2,1,0:T(8,128)S(1)} %get-tuple-element.15), channel_id=1, source_target_pairs={{0,24},{1,25},{2,26},{3,27},{4,28},{5,29},{6,30},{7,31},{8,0},{9,1... | collective-permute-start | bytes 147464 | tf_op jit(solution)/shard_map/ppermute | solution.py:179
  36.2 0.8 %dynamic-slice_convert_fusion = f32[720]{0:T(1024)S(1)} fusion(s32[23040]{0:T(1024)} %param.7, s32[]{:T(128)S(6)} %select_n.73), kind=kLoop, calls=%fused_computation.22 | loop fusion | flops 720 | bytes 5764 | tf_op jit(solution)/shard_map/convert_element_type | solution.py:169
  37.0 0.6 %broadcast_in_dim.28.mask_ref = f32[1,720]{1,0:T(1,128)} reshape(f32[720]{0:T(1024)S(1)} %dynamic-slice_convert_fusion) | data formatting | bytes 5760 | tf_op jit(solution)/shard_map/broadcast_in_dim | solution.py:193
  37.6 0.6 %pad.10.clone.inv_ref = f32[16,16]{1,0:T(8,128)} pad(f32[13,13]{1,0:T(8,128)S(1)} %copy.13, f32[]{:T(128)} %constant.167.clone.1), padding=0_3x0_3 | pad | bytes 1704 | tf_op jit(solution)/shard_map/jit(_pad)/pad | solution.py:167
  38.2 0.4 collective-permute-done.5.refs_2_
  38.7 0.4 collective-permute-done.6.refs_3_
  39.1 0.2 copy-done.1
  39.3 0.4 copy-done.2
  39.7 1.9 %fit.1 = (f32[13,720]{1,0:T(8,128)}, f32[1,720]{1,0:T(1,128)}) custom-call(f32[16,16]{1,0:T(8,128)} %pad.10.clone.inv_ref, f32[16,16]{1,0:T(8,128)} %pad_bitcast_fusion.invt_ref, f32[1,720]{1,0:T(1,128)} %broadcast_in_dim.28.mask_ref, f32[1,16,768]{2,1,0:T(8,128)} %get-tuple-element.18.refs_0_, f32[1,16,768]{2,1,0:T(8,128)} %copy-done, ...), custom_call_target="tpu_custom_call" | custom-call | tf_op jit(solution)/shard_map/fit/pallas_call | solution.py:186
  41.6 1.3 %reduce.6 = f32[720]{0:T(1024)} reduce(f32[1,720]{1,0:T(1,128)} %get-tuple-element.9, f32[]{:T(128)} %constant.191), dimensions={0}, to_apply=%get-tuple-element.9.reduce_sub_computation | reduce | bytes 5764 | tf_op jit(solution)/shard_map/fit/pallas_call | solution.py:186
  (26 shorter events, 0.9 us)
Async XLA Ops:
  0.6 10.3 %copy-start.3 = (s32[1024]{0:T(1024)S(1)}, s32[1024]{0:T(1024)}, u32[]{:S(2)}) copy-start(s32[1024]{0:T(1024)} %param.5) | copy-start | bytes 12292
  3.8 18.2 %copy-start.4 = (s32[32]{0:T(128)S(1)}, s32[32]{0:T(128)}, u32[]{:S(2)}) copy-start(s32[32]{0:T(128)} %param.6) | copy-start | bytes 388
  10.4 4.8 %collective-permute-start = (f32[16,16,768]{2,1,0:T(8,128)}, f32[16,16,768]{2,1,0:T(8,128)S(1)}, u32[]{:S(2)}, u32[]{:S(2)}) collective-permute-start(f32[16,16,768]{2,1,0:T(8,128)} %get-tuple-element.7), channel_id=1, source_target_pairs={{0,1},{1,0},{2,3},{3,2},{4,5},{5,4},{6,7},{7,6},{8,9},{9,8},{10,11... | collective-permute-start | bytes 2359304 | tf_op jit(solution)/shard_map/ppermute | solution.py:179
  16.4 9.3 %collective-permute-start.1 = (f32[4,16,768]{2,1,0:T(8,128)S(1)}, f32[4,16,768]{2,1,0:T(8,128)S(1)}, u32[]{:S(2)}, u32[]{:S(2)}) collective-permute-start(f32[4,16,768]{2,1,0:T(8,128)S(1)} %get-tuple-element.12), channel_id=1, source_target_pairs={{0,2},{1,3},{2,4},{3,5},{4,6},{5,7},{6,0},{7,1},{8,10},{9,11},{10,... | collective-permute-start | bytes 589832 | tf_op jit(solution)/shard_map/ppermute | solution.py:179
  19.0 10.7 %collective-permute-start.2 = (f32[4,16,768]{2,1,0:T(8,128)S(1)}, f32[4,16,768]{2,1,0:T(8,128)S(1)}, u32[]{:S(2)}, u32[]{:S(2)}) collective-permute-start(f32[4,16,768]{2,1,0:T(8,128)S(1)} %get-tuple-element.14), channel_id=1, source_target_pairs={{0,4},{1,5},{2,6},{3,7},{4,0},{5,1},{6,2},{7,3},{8,12},{9,13},{10,... | collective-permute-start | bytes 589832 | tf_op jit(solution)/shard_map/ppermute | solution.py:179
  20.5 9.5 %collective-permute-start.3 = (f32[4,16,768]{2,1,0:T(8,128)S(1)}, f32[4,16,768]{2,1,0:T(8,128)S(1)}, u32[]{:S(2)}, u32[]{:S(2)}) collective-permute-start(f32[4,16,768]{2,1,0:T(8,128)S(1)} %get-tuple-element.13), channel_id=1, source_target_pairs={{0,6},{1,7},{2,0},{3,1},{4,2},{5,3},{6,4},{7,5},{8,14},{9,15},{10,... | collective-permute-start | bytes 589832 | tf_op jit(solution)/shard_map/ppermute | solution.py:179
  30.7 7.6 %collective-permute-start.4 = (f32[1,16,768]{2,1,0:T(8,128)S(1)}, f32[1,16,768]{2,1,0:T(8,128)S(1)}, u32[]{:S(2)}, u32[]{:S(2)}) collective-permute-start(f32[1,16,768]{2,1,0:T(8,128)S(1)} %get-tuple-element.17), channel_id=1, source_target_pairs={{0,8},{1,9},{2,10},{3,11},{4,12},{5,13},{6,14},{7,15},{8,16},{9,17... | collective-permute-start | bytes 147464 | tf_op jit(solution)/shard_map/ppermute | solution.py:179
  32.2 6.4 %collective-permute-start.5 = (f32[1,16,768]{2,1,0:T(8,128)S(1)}, f32[1,16,768]{2,1,0:T(8,128)S(1)}, u32[]{:S(2)}, u32[]{:S(2)}) collective-permute-start(f32[1,16,768]{2,1,0:T(8,128)S(1)} %get-tuple-element.16), channel_id=1, source_target_pairs={{0,16},{1,17},{2,18},{3,19},{4,20},{5,21},{6,22},{7,23},{8,24},{9,... | collective-permute-start | bytes 147464 | tf_op jit(solution)/shard_map/ppermute | solution.py:179
  34.8 4.2 %collective-permute-start.6 = (f32[1,16,768]{2,1,0:T(8,128)S(1)}, f32[1,16,768]{2,1,0:T(8,128)S(1)}, u32[]{:S(2)}, u32[]{:S(2)}) collective-permute-start(f32[1,16,768]{2,1,0:T(8,128)S(1)} %get-tuple-element.15), channel_id=1, source_target_pairs={{0,24},{1,25},{2,26},{3,27},{4,28},{5,29},{6,30},{7,31},{8,0},{9,1... | collective-permute-start | bytes 147464 | tf_op jit(solution)/shard_map/ppermute | solution.py:179
  38.2 0.8 %copy-start = (f32[1,16,768]{2,1,0:T(8,128)}, f32[1,16,768]{2,1,0:T(8,128)S(1)}, u32[]{:S(2)}) copy-start(f32[1,16,768]{2,1,0:T(8,128)S(1)} %collective-permute-done.4.refs_1_) | copy-start | bytes 147460
  38.7 0.6 %copy-start.1 = (f32[1,16,768]{2,1,0:T(8,128)}, f32[1,16,768]{2,1,0:T(8,128)S(1)}, u32[]{:S(2)}) copy-start(f32[1,16,768]{2,1,0:T(8,128)S(1)} %collective-permute-done.5.refs_2_) | copy-start | bytes 147460
  39.1 0.6 %copy-start.2 = (f32[1,16,768]{2,1,0:T(8,128)}, f32[1,16,768]{2,1,0:T(8,128)S(1)}, u32[]{:S(2)}) copy-start(f32[1,16,768]{2,1,0:T(8,128)S(1)} %collective-permute-done.6.refs_3_) | copy-start | bytes 147460

commit v2 on v1

v2 whole, which is shorter than its diff:
```python
import functools
import math

import jax
import jax.numpy as jnp
from jax import lax
from jax.experimental import pallas as pl
from jax.experimental.pallas import tpu as pltpu
from jax.sharding import PartitionSpec as P

HARMS = 6
LANES = 128
ROWS = 16


def harmonic_basis(day_values):
    angles = day_values.astype(jnp.float32) * (2.0 * math.pi / 365.0)
    basis_rows = [jnp.ones_like(angles)]
    for order in range(1, HARMS + 1):
        basis_rows.append(jnp.cos(order * angles))
        basis_rows.append(jnp.sin(order * angles))
    return jnp.stack(basis_rows, 0)


def split_radices(groups):
    radices = []
    rest = groups
    if rest % 2 == 0:
        radices.append(2)
        rest //= 2
    while rest % 4 == 0:
        radices.append(4)
        rest //= 4
    if rest > 1 or not radices:
        radices.append(rest)
    return radices


def round_up(value, unit):
    return -(-value // unit) * unit


def chunk_of(cells, most):
    tiles = cells // LANES
    best = max(t for t in range(1, tiles + 1) if tiles % t == 0 and t * LANES <= most)
    return best * LANES


def split_design(days, steps_dev, cols):
    lanes = days.shape[1]
    lane = lax.broadcasted_iota(jnp.int32, (ROWS, lanes), 1)
    row = lax.broadcasted_iota(jnp.int32, (ROWS, lanes), 0)
    angles = days * (2.0 * math.pi / 365.0)
    multiple = ((row + 1) // 2).astype(jnp.float32)
    argument = multiple * angles
    design = jnp.where(row % 2 == 1, jnp.cos(argument), jnp.sin(argument))
    design = jnp.where(row == 0, 1.0, design)
    design = jnp.where((row < cols) & (lane < 3 * steps_dev), design, 0.0)
    high = design.astype(jnp.bfloat16).astype(jnp.float32)
    mid = (design - high).astype(jnp.bfloat16).astype(jnp.float32)
    low = design - high - mid
    mid = jnp.where(lane < 2 * steps_dev, mid, 0.0)
    low = jnp.where(lane < steps_dev, low, 0.0)
    return jnp.concatenate([high, mid, low], 0).astype(jnp.bfloat16)


def own_days(days_ref, own_index, steps_dev):
    lanes = round_up(3 * steps_dev, LANES)
    start = own_index * steps_dev
    offset = lax.rem(start, LANES)
    window = days_ref[:, pl.ds(pl.multiple_of(start - offset, LANES), LANES)]
    window = jnp.broadcast_to(window.astype(jnp.float32), (ROWS, LANES))
    first = pltpu.roll(window, lax.rem(LANES - offset, LANES), 1)
    lane = lax.broadcasted_iota(jnp.int32, (ROWS, LANES), 1)
    second = pltpu.roll(first, steps_dev, 1)
    third = pltpu.roll(first, 2 * steps_dev, 1)
    days = jnp.where(lane < steps_dev, first, jnp.where(lane < 2 * steps_dev, second, third))
    return days[:, :lanes]


def sums_kernel(
    owner_ref, days_ref, field_ref, *refs, cols, band, width, chunk, lead, steps_dev, radices
):
    outs, lhs_ref, scratch = refs[:-2], refs[-2], refs[-1]
    step = pl.program_id(0)
    own_index = lax.axis_index("span")

    @pl.when(step == 0)
    def _():
        days = own_days(days_ref, own_index, steps_dev)
        lhs_ref[...] = split_design(days, steps_dev, cols)

    f = field_ref[...]
    high = f.astype(jnp.bfloat16)
    left = f - high.astype(jnp.float32)
    mid = left.astype(jnp.bfloat16)
    low = (left - mid.astype(jnp.float32)).astype(jnp.bfloat16)
    stacked = jnp.concatenate([high, mid, low], 0)
    parts = jnp.dot(
        lhs_ref[:, : 3 * steps_dev], stacked, preferred_element_type=jnp.float32
    )
    total = parts[:ROWS] + (parts[ROWS : 2 * ROWS] + parts[2 * ROWS :])
    squares = jnp.sum(f * f, axis=0, keepdims=True)
    row = lax.broadcasted_iota(jnp.int32, total.shape, 0)
    scratch[:, pl.ds(pl.multiple_of(step * chunk, LANES), chunk)] = jnp.where(
        row == cols, squares, total
    )

    @pl.when(step == pl.num_programs(0) - 1)
    def _():
        edge = scratch.shape[1] - 2 * LANES
        scratch[:, edge:] = jnp.zeros((ROWS, 2 * LANES), jnp.float32)
        for q in range(lead * len(outs)):
            start = q * band
            offset = start % LANES
            base = start - offset
            if offset:
                span = width + LANES
                block = pltpu.roll(scratch[:, base : base + span], span - offset, 1)[:, :width]
            else:
                block = scratch[:, base : base + width]
            target, source = owner_ref[q], own_index
            place, inner, first = 0, lead, None
            for radix in radices:
                digit = lax.rem(lax.rem(target, radix) - lax.rem(source, radix) + radix, radix)
                target, source = lax.div(target, radix), lax.div(source, radix)
                if first is None:
                    first = digit
                else:
                    inner //= radix
                    place = place + digit * inner
            for k, out in enumerate(outs):

                @pl.when(first == k)
                def _(out=out, block=block, place=place):
                    out[place] = block


def on_device(field, day_table, band_owner, sea_mask):
    groups = lax.axis_size("span")
    own_index = lax.axis_index("span")
    steps_dev, cells = field.shape
    band = cells // groups
    width = round_up(band, LANES)
    steps = day_table.shape[0]
    radices = split_radices(groups)
    strides = [math.prod(radices[:r]) for r in range(len(radices))]

    cols = 2 * HARMS + 1
    lead = groups // radices[0]
    chunk = chunk_of(cells, 4608)
    lanes = round_up(3 * steps_dev, LANES)
    pieces = pl.pallas_call(
        functools.partial(
            sums_kernel,
            cols=cols,
            band=band,
            width=width,
            chunk=chunk,
            lead=lead,
            steps_dev=steps_dev,
            radices=radices,
        ),
        grid_spec=pltpu.PrefetchScalarGridSpec(
            num_scalar_prefetch=1,
            grid=(cells // chunk,),
            in_specs=[
                pl.BlockSpec((1, steps), lambda s, o: (0, 0)),
                pl.BlockSpec((steps_dev, chunk), lambda s, o: (0, s)),
            ],
            out_specs=[pl.BlockSpec((lead, ROWS, width), lambda s, o: (0, 0, 0))] * radices[0],
            scratch_shapes=[
                pltpu.VMEM((3 * ROWS, lanes), jnp.bfloat16),
                pltpu.VMEM((ROWS, cells + 2 * LANES), jnp.float32),
            ],
        ),
        out_shape=[jax.ShapeDtypeStruct((lead, ROWS, width), jnp.float32)] * radices[0],
        name="sums",
    )(band_owner, day_table[None, :], field)

    slots = jnp.arange(groups, dtype=jnp.int32)
    pieces = list(pieces)
    for r, (radix, stride) in enumerate(zip(radices, strides)):
        received = []
        for shift in range(1, radix):
            pairs = []
            for source in range(groups):
                digit = source // stride % radix
                pairs.append((source, source + ((digit + shift) % radix - digit) * stride))
            received.append(lax.ppermute(pieces[shift], "span", pairs))
        pieces = [pieces[0]] + received
        total = functools.reduce(jnp.add, pieces)
        if r == 0:
            late_days, total = lax.optimization_barrier((day_table, total))
        if r + 1 < len(radices):
            part = total.shape[0] // radices[r + 1]
            pieces = [total[k * part : (k + 1) * part] for k in range(radices[r + 1])]

    design = harmonic_basis(late_days)
    gram = jnp.dot(design, design.T, precision=lax.Precision.HIGHEST)
    factor = jnp.linalg.cholesky(gram)
    inverse = lax.linalg.triangular_solve(
        factor, jnp.eye(cols, dtype=jnp.float32), left_side=True, lower=True
    )
    own_band = jnp.sum(jnp.where(band_owner == own_index, slots, 0))
    mask = lax.dynamic_slice_in_dim(sea_mask, own_band * band, band).astype(jnp.float32)

    total = total[0, :, :band]
    half = jnp.dot(inverse, total[:cols], precision=lax.Precision.HIGHEST)
    coeffs = jnp.dot(inverse.T, half, precision=lax.Precision.HIGHEST)
    rest = total[cols] - jnp.sum(half * half, axis=0)
    variance = jnp.maximum(rest, 0.0) / steps
    return (coeffs * mask[None, :], variance * mask)


def solution(mesh):
    in_specs = (P(("member", "span"), None), P("member"), P("member"), P())
    out_specs = (P(None, ("member", "span")), P(("member", "span")))
    return jax.shard_map(
        on_device, mesh=mesh, in_specs=in_specs, out_specs=out_specs, check_vma=False
    )
```

time: 43.3 us -> 38.1 us (0.88)
  other arithmetic: 10.6 us -> 6.9 us
  local copies, waits for them, and re-layouts: 3.46 us -> 0.31 us
  matrix products: 0.37 us -> 1.42 us
    pallas_call x1, Pallas kernels: 6.62 us -> 8.66 us  [on_device(): pl.pallas_call(functools.partial(sums_kernel, cols=cols, band=band, width...]
    pallas_call x1 -> x0, Pallas kernels: 1.91 us -> none  [on_device(): pl.pallas_call(functools.partial(fit_kernel, cols=cols, band=band, steps=...]
    mul x0 -> x1, other arithmetic: none -> 1.37 us  [on_device(): return (coeffs * mask[None, :], variance * mask)]
    reduce_sum x1 -> x0, other arithmetic: 1.35 us -> none  [on_device(): jnp.sum(jnp.where(band_owner[None, :] == target[:, None], slots[None, :],...]
    pallas_call x1 -> x0, other arithmetic: 1.28 us -> none  [on_device(): pl.pallas_call(functools.partial(fit_kernel, cols=cols, band=band, steps=...]
    dot_general x0 -> x2, matrix products: none -> 1.06 us  [the longest x1 0.87 us: on_device(): coeffs = jnp.dot(inverse.T, half, precision=lax.Precision.HIGHEST)]
    another operation x3 -> x0, other arithmetic: 0.97 us -> none  [the longest x2 0.96 us: harmonic_basis(): return jnp.stack(basis_rows, 0)]
    convert_element_type x1 -> x0, other arithmetic: 0.77 us -> none  [on_device(): lax.dynamic_slice_in_dim(sea_mask, own_band * band, band)]
  transfers between devices with their start and end apart: 7 -> 7, of which waited for: 5 -> 6; matrix products, arithmetic and copies ran while one was open for 17% -> 13% of each run, Pallas kernels for 0% -> 0%
where the time goes in v2:
time: 38.1 us; the launch traced here: 37.8 us
  starting transfers between devices  11.9 us (31%)
  Pallas kernels  8.66 us (23%)
  waiting for transfers between devices  7.16 us (19%)
  other arithmetic  6.9 us (18%)
  matrix products  1.42 us (4%)
  between operations  1.38 us (4%)
    ppermute x7, starting transfers between devices, on_device(): received.append(lax.ppermute(pieces[shift], 'span', pairs))  11.9 us
    pallas_call x1, Pallas kernels, on_device(): pl.pallas_call(functools.partial(sums_kernel, cols=cols, band=band, width...  8.66 us
    ppermute x7, waiting for transfers between devices, on_device(): received.append(lax.ppermute(pieces[shift], 'span', pairs))  7.16 us
    another operation x3, other arithmetic, on_device(): factor = jnp.linalg.cholesky(gram)  1.87 us
    another operation x2, other arithmetic, on_device(): lax.linalg.triangular_solve(factor, jnp.eye(cols, dtype=jnp.float32), lef...  1.65 us
    mul x1, other arithmetic, on_device(): return (coeffs * mask[None, :], variance * mask)  1.37 us
    add x3, other arithmetic, on_device(): total = functools.reduce(jnp.add, pieces)  1.27 us
    dot_general x1, matrix products, on_device(): coeffs = jnp.dot(inverse.T, half, precision=lax.Precision.HIGHEST)  0.87 us
  transfers between devices with their start and end apart: 7, of which 6 were waited for; matrix products, arithmetic and copies ran while one was open for 13% of the time, Pallas kernels for 0%

profile of v2, /device:TPU:0, one launch (start us, length us, event | category | flops | bytes accessed | tf_op | source)
XLA Modules:
  0.0 37.8 jit_solution(17443436547154491656)
XLA Ops:
  0.6 0.0 copy-start.1
  0.6 0.0 copy-start
  0.7 8.7 %sums.1 = (f32[16,16,768]{2,1,0:T(8,128)}, f32[16,16,768]{2,1,0:T(8,128)}) custom-call(s32[32]{0:T(128)} %owner_ref.1, s32[1,1024]{1,0:T(1,128)} %bitcast.32, f32[32,23040]{1,0:T(8,128)} %field_ref.1), custom_call_target="tpu_custom_call" | custom-call | tf_op jit(solution)/shard_map/sums/pallas_call | solution.py:153
  9.3 0.5 %collective-permute-start = (f32[16,16,768]{2,1,0:T(8,128)}, f32[16,16,768]{2,1,0:T(8,128)S(1)}, u32[]{:S(2)}, u32[]{:S(2)}) collective-permute-start(f32[16,16,768]{2,1,0:T(8,128)} %get-tuple-element.7), channel_id=1, source_target_pairs={{0,1},{1,0},{2,3},{3,2},{4,5},{5,4},{6,7},{7,6},{8,9},{9,8},{10,11... | collective-permute-start | bytes 2359304 | tf_op jit(solution)/shard_map/ppermute | solution.py:190
  9.8 0.0 copy-done.1
  9.8 0.6 %fusion.19 = s32[]{:T(128)} fusion(s32[32]{0:T(128)S(1)} %copy-done.1, s32[]{:T(128)S(6)} %axis_index.12), kind=kLoop, calls=%fused_computation.40 | loop fusion | flops 95 | bytes 136 | tf_op jit(solution)/shard_map/reduce_sum | solution.py:205
  11.1 0.8 %collective-permute-done = f32[16,16,768]{2,1,0:T(8,128)S(1)} collective-permute-done((f32[16,16,768]{2,1,0:T(8,128)}, f32[16,16,768]{2,1,0:T(8,128)S(1)}, u32[]{:S(2)}, u32[]{:S(2)}) %collective-permute-start) | collective-permute-done | bytes 786464 | tf_op jit(solution)/shard_map/ppermute | solution.py:190
  11.9 1.2 %add.35 = f32[16,16,768]{2,1,0:T(8,128)S(1)} add(f32[16,16,768]{2,1,0:T(8,128)} %get-tuple-element.6, f32[16,16,768]{2,1,0:T(8,128)S(1)} %collective-permute-done) | non-fusion elementwise | flops 196608 | bytes 2359296 | tf_op jit(solution)/shard_map/add | solution.py:192
  13.2 2.9 %collective-permute-start.1 = (f32[4,16,768]{2,1,0:T(8,128)S(1)}, f32[4,16,768]{2,1,0:T(8,128)S(1)}, u32[]{:S(2)}, u32[]{:S(2)}) collective-permute-start(f32[4,16,768]{2,1,0:T(8,128)S(1)} %get-tuple-element.12), channel_id=1, source_target_pairs={{0,2},{1,3},{2,4},{3,5},{4,6},{5,7},{6,0},{7,1},{8,10},{9,11},{10,... | collective-permute-start | bytes 589832 | tf_op jit(solution)/shard_map/ppermute | solution.py:190
  16.1 1.5 %collective-permute-start.2 = (f32[4,16,768]{2,1,0:T(8,128)S(1)}, f32[4,16,768]{2,1,0:T(8,128)S(1)}, u32[]{:S(2)}, u32[]{:S(2)}) collective-permute-start(f32[4,16,768]{2,1,0:T(8,128)S(1)} %get-tuple-element.14), channel_id=1, source_target_pairs={{0,4},{1,5},{2,6},{3,7},{4,0},{5,1},{6,2},{7,3},{8,12},{9,13},{10,... | collective-permute-start | bytes 589832 | tf_op jit(solution)/shard_map/ppermute | solution.py:190
  17.6 1.4 %collective-permute-start.3 = (f32[4,16,768]{2,1,0:T(8,128)S(1)}, f32[4,16,768]{2,1,0:T(8,128)S(1)}, u32[]{:S(2)}, u32[]{:S(2)}) collective-permute-start(f32[4,16,768]{2,1,0:T(8,128)S(1)} %get-tuple-element.13), channel_id=1, source_target_pairs={{0,6},{1,7},{2,0},{3,1},{4,2},{5,3},{6,4},{7,5},{8,14},{9,15},{10,... | collective-permute-start | bytes 589832 | tf_op jit(solution)/shard_map/ppermute | solution.py:190
  19.1 0.1 fusion.17
  19.2 0.1 stack.51
  19.3 0.2 fusion.22
  19.4 0.1 copy.6
  19.6 1.2 %cholesky.17 = f32[13,13]{1,0:T(8,128)S(1)} custom-call(f32[13,13]{1,0:T(8,128)S(1)} %fusion.6), custom_call_target="Cholesky" | custom-call | tf_op jit(solution)/shard_map/jit(cholesky)/cholesky | solution.py:201
  20.8 0.6 %compare_reduce_fusion = pred[]{:T(512)} fusion(f32[13]{0:T(128)S(1)} %select_reduce_fusion), kind=kLoop, calls=%fused_computation.39 | loop fusion | flops 25 | bytes 53 | tf_op jit(solution)/shard_map/jit(cholesky)/cholesky | solution.py:201
  21.5 0.6 %fusion.3 = f32[1,13,13]{2,1,0:T(8,128)S(1)} fusion(f32[13,13]{1,0:T(8,128)S(1)} %cholesky.17, pred[]{:T(512)} %compare_reduce_fusion), kind=kLoop, calls=%fused_computation.9 | loop fusion | flops 676 | bytes 1353 | tf_op jit(solution)/shard_map/triangular_solve | solution.py:202
  22.1 1.0 %custom-call.6 = f32[1,13,13]{1,2,0:T(8,128)S(1)} custom-call(f32[1,13,13]{2,1,0:T(8,128)S(1)} %fusion.3), custom_call_target="InvertDiagBlocksLowerTriangular" | custom-call | tf_op jit(solution)/shard_map/triangular_solve | solution.py:202
  23.1 0.0 collective-permute-done.1
  23.1 3.4 %collective-permute-done.2 = f32[4,16,768]{2,1,0:T(8,128)S(1)} collective-permute-done((f32[4,16,768]{2,1,0:T(8,128)S(1)}, f32[4,16,768]{2,1,0:T(8,128)S(1)}, u32[]{:S(2)}, u32[]{:S(2)}) %collective-permute-start.2) | collective-permute-done | bytes 196640 | tf_op jit(solution)/shard_map/ppermute | solution.py:190
  26.5 0.3 collective-permute-done.3
  26.8 1.6 %collective-permute-start.4 = (f32[1,16,768]{2,1,0:T(8,128)S(1)}, f32[1,16,768]{2,1,0:T(8,128)S(1)}, u32[]{:S(2)}, u32[]{:S(2)}) collective-permute-start(f32[1,16,768]{2,1,0:T(8,128)S(1)} %get-tuple-element.15), channel_id=1, source_target_pairs={{0,8},{1,9},{2,10},{3,11},{4,12},{5,13},{6,14},{7,15},{8,16},{9,17... | collective-permute-start | bytes 147464 | tf_op jit(solution)/shard_map/ppermute | solution.py:190
  28.5 2.6 %collective-permute-start.5 = (f32[1,16,768]{2,1,0:T(8,128)S(1)}, f32[1,16,768]{2,1,0:T(8,128)S(1)}, u32[]{:S(2)}, u32[]{:S(2)}) collective-permute-start(f32[1,16,768]{2,1,0:T(8,128)S(1)} %get-tuple-element.17), channel_id=1, source_target_pairs={{0,16},{1,17},{2,18},{3,19},{4,20},{5,21},{6,22},{7,23},{8,24},{9,... | collective-permute-start | bytes 147464 | tf_op jit(solution)/shard_map/ppermute | solution.py:190
  31.1 1.4 %collective-permute-start.6 = (f32[1,16,768]{2,1,0:T(8,128)S(1)}, f32[1,16,768]{2,1,0:T(8,128)S(1)}, u32[]{:S(2)}, u32[]{:S(2)}) collective-permute-start(f32[1,16,768]{2,1,0:T(8,128)S(1)} %get-tuple-element.16), channel_id=1, source_target_pairs={{0,24},{1,25},{2,26},{3,27},{4,28},{5,29},{6,30},{7,31},{8,0},{9,1... | collective-permute-start | bytes 147464 | tf_op jit(solution)/shard_map/ppermute | solution.py:190
  32.4 0.2 fusion.4
  32.6 0.3 collective-permute-done.4
  32.9 1.9 %collective-permute-done.5 = f32[1,16,768]{2,1,0:T(8,128)S(1)} collective-permute-done((f32[1,16,768]{2,1,0:T(8,128)S(1)}, f32[1,16,768]{2,1,0:T(8,128)S(1)}, u32[]{:S(2)}, u32[]{:S(2)}) %collective-permute-start.5) | collective-permute-done | bytes 49184 | tf_op jit(solution)/shard_map/ppermute | solution.py:190
  34.9 0.4 %collective-permute-done.6 = f32[1,16,768]{2,1,0:T(8,128)S(1)} collective-permute-done((f32[1,16,768]{2,1,0:T(8,128)S(1)}, f32[1,16,768]{2,1,0:T(8,128)S(1)}, u32[]{:S(2)}, u32[]{:S(2)}) %collective-permute-start.6) | collective-permute-done | bytes 49184 | tf_op jit(solution)/shard_map/ppermute | solution.py:190
  35.3 0.2 multiply_reduce_fusion
  35.5 1.4 %multiply_multiply_fusion = (f32[720]{0:T(1024)}, f32[720]{0:T(1024)S(1)}) fusion(f32[720]{0:T(1024)S(1)} %slice_reduce_fusion, f32[720]{0:T(1024)S(1)} %get-tuple-element.30, s32[23040]{0:T(1024)} %param.7, s32[]{:T(128)S(6)} %select_n.13), kind=kLoop, calls=%fused_computation.17 | loop fusion | flops 3600 | bytes 14404 | tf_op jit(solution)/shard_map/mul | solution.py:213
  36.9 0.9 %convolution_multiply_fusion = f32[13,720]{1,0:T(8,128)} fusion(f32[13,13]{1,0:T(8,128)S(1)} %fusion.4, f32[13,720]{1,0:T(8,128)S(1)} %get-tuple-element.31, f32[720]{0:T(1024)S(1)} %get-tuple-element.11), kind=kOutput, calls=%fused_computation | convolution fusion | flops 1469520 | bytes 78436 | tf_op jit(solution)/shard_map/dot_general | solution.py:210
  (9 shorter events, 0.2 us)
Async XLA Ops:
  0.6 9.2 %copy-start.1 = (s32[32]{0:T(128)S(1)}, s32[32]{0:T(128)}, u32[]{:S(2)}) copy-start(s32[32]{0:T(128)} %owner_ref.1) | copy-start | bytes 388
  0.6 18.4 %copy-start = (s32[1024]{0:T(1024)S(1)}, s32[1024]{0:T(1024)}, u32[]{:S(2)}) copy-start(s32[1024]{0:T(1024)} %param.5) | copy-start | bytes 12292
  9.3 2.6 %collective-permute-start = (f32[16,16,768]{2,1,0:T(8,128)}, f32[16,16,768]{2,1,0:T(8,128)S(1)}, u32[]{:S(2)}, u32[]{:S(2)}) collective-permute-start(f32[16,16,768]{2,1,0:T(8,128)} %get-tuple-element.7), channel_id=1, source_target_pairs={{0,1},{1,0},{2,3},{3,2},{4,5},{5,4},{6,7},{7,6},{8,9},{9,8},{10,11... | collective-permute-start | bytes 2359304 | tf_op jit(solution)/shard_map/ppermute | solution.py:190
  13.2 9.9 %collective-permute-start.1 = (f32[4,16,768]{2,1,0:T(8,128)S(1)}, f32[4,16,768]{2,1,0:T(8,128)S(1)}, u32[]{:S(2)}, u32[]{:S(2)}) collective-permute-start(f32[4,16,768]{2,1,0:T(8,128)S(1)} %get-tuple-element.12), channel_id=1, source_target_pairs={{0,2},{1,3},{2,4},{3,5},{4,6},{5,7},{6,0},{7,1},{8,10},{9,11},{10,... | collective-permute-start | bytes 589832 | tf_op jit(solution)/shard_map/ppermute | solution.py:190
  16.1 10.4 %collective-permute-start.2 = (f32[4,16,768]{2,1,0:T(8,128)S(1)}, f32[4,16,768]{2,1,0:T(8,128)S(1)}, u32[]{:S(2)}, u32[]{:S(2)}) collective-permute-start(f32[4,16,768]{2,1,0:T(8,128)S(1)} %get-tuple-element.14), channel_id=1, source_target_pairs={{0,4},{1,5},{2,6},{3,7},{4,0},{5,1},{6,2},{7,3},{8,12},{9,13},{10,... | collective-permute-start | bytes 589832 | tf_op jit(solution)/shard_map/ppermute | solution.py:190
  17.6 9.1 %collective-permute-start.3 = (f32[4,16,768]{2,1,0:T(8,128)S(1)}, f32[4,16,768]{2,1,0:T(8,128)S(1)}, u32[]{:S(2)}, u32[]{:S(2)}) collective-permute-start(f32[4,16,768]{2,1,0:T(8,128)S(1)} %get-tuple-element.13), channel_id=1, source_target_pairs={{0,6},{1,7},{2,0},{3,1},{4,2},{5,3},{6,4},{7,5},{8,14},{9,15},{10,... | collective-permute-start | bytes 589832 | tf_op jit(solution)/shard_map/ppermute | solution.py:190
  26.8 6.1 %collective-permute-start.4 = (f32[1,16,768]{2,1,0:T(8,128)S(1)}, f32[1,16,768]{2,1,0:T(8,128)S(1)}, u32[]{:S(2)}, u32[]{:S(2)}) collective-permute-start(f32[1,16,768]{2,1,0:T(8,128)S(1)} %get-tuple-element.15), channel_id=1, source_target_pairs={{0,8},{1,9},{2,10},{3,11},{4,12},{5,13},{6,14},{7,15},{8,16},{9,17... | collective-permute-start | bytes 147464 | tf_op jit(solution)/shard_map/ppermute | solution.py:190
  28.5 6.4 %collective-permute-start.5 = (f32[1,16,768]{2,1,0:T(8,128)S(1)}, f32[1,16,768]{2,1,0:T(8,128)S(1)}, u32[]{:S(2)}, u32[]{:S(2)}) collective-permute-start(f32[1,16,768]{2,1,0:T(8,128)S(1)} %get-tuple-element.17), channel_id=1, source_target_pairs={{0,16},{1,17},{2,18},{3,19},{4,20},{5,21},{6,22},{7,23},{8,24},{9,... | collective-permute-start | bytes 147464 | tf_op jit(solution)/shard_map/ppermute | solution.py:190
  31.1 4.2 %collective-permute-start.6 = (f32[1,16,768]{2,1,0:T(8,128)S(1)}, f32[1,16,768]{2,1,0:T(8,128)S(1)}, u32[]{:S(2)}, u32[]{:S(2)}) collective-permute-start(f32[1,16,768]{2,1,0:T(8,128)S(1)} %get-tuple-element.16), channel_id=1, source_target_pairs={{0,24},{1,25},{2,26},{3,27},{4,28},{5,29},{6,30},{7,31},{8,0},{9,1... | collective-permute-start | bytes 147464 | tf_op jit(solution)/shard_map/ppermute | solution.py:190

commit v3 on v2

v3 whole, which is shorter than its diff:
```python
import functools
import math

import jax
import jax.numpy as jnp
from jax import lax
from jax.experimental import pallas as pl
from jax.experimental.pallas import tpu as pltpu
from jax.sharding import PartitionSpec as P

HARMS = 6
LANES = 128
ROWS = 16


def sine_of_turns(turns):
    turns = turns - jnp.floor(turns + 0.5)
    turns = jnp.where(turns > 0.25, 0.5 - turns, jnp.where(turns < -0.25, -0.5 - turns, turns))
    x = turns * (2.0 * math.pi)
    square = x * x
    value = jnp.full_like(x, 1.0 / math.factorial(13))
    for power in (11, 9, 7, 5, 3, 1):
        value = value * square + (-1.0) ** (power // 2) / math.factorial(power)
    return value * x


def basis_rows(days, rows):
    row = lax.broadcasted_iota(jnp.int32, (rows, days.shape[-1]), 0)
    multiple = ((row + 1) // 2).astype(jnp.float32)
    whole = multiple * days
    whole = whole - 365.0 * jnp.floor(whole * (1.0 / 365.0))
    quarter = jnp.where(row % 2 == 1, 0.25, 0.0)
    values = sine_of_turns(whole * (1.0 / 365.0) + quarter)
    return jnp.where(row == 0, 1.0, values)


def split_radices(groups):
    radices = []
    rest = groups
    if rest % 2 == 0:
        radices.append(2)
        rest //= 2
    while rest % 4 == 0:
        radices.append(4)
        rest //= 4
    if rest > 1 or not radices:
        radices.append(rest)
    return radices


def round_up(value, unit):
    return -(-value // unit) * unit


def chunk_of(cells, most):
    tiles = cells // LANES
    best = max(t for t in range(1, tiles + 1) if tiles % t == 0 and t * LANES <= most)
    return best * LANES


def split_design(days, steps_dev, cols):
    lanes = days.shape[1]
    lane = lax.broadcasted_iota(jnp.int32, (ROWS, lanes), 1)
    row = lax.broadcasted_iota(jnp.int32, (ROWS, lanes), 0)
    design = basis_rows(days, ROWS)
    design = jnp.where((row < cols) & (lane < 3 * steps_dev), design, 0.0)
    high = design.astype(jnp.bfloat16).astype(jnp.float32)
    mid = (design - high).astype(jnp.bfloat16).astype(jnp.float32)
    low = design - high - mid
    mid = jnp.where(lane < 2 * steps_dev, mid, 0.0)
    low = jnp.where(lane < steps_dev, low, 0.0)
    return jnp.concatenate([high, mid, low], 0).astype(jnp.bfloat16)


def own_days(days_ref, own_index, steps_dev):
    lanes = round_up(3 * steps_dev, LANES)
    start = own_index * steps_dev
    offset = lax.rem(start, LANES)
    window = days_ref[:, pl.ds(pl.multiple_of(start - offset, LANES), LANES)]
    window = jnp.broadcast_to(window.astype(jnp.float32), (ROWS, LANES))
    first = pltpu.roll(window, lax.rem(LANES - offset, LANES), 1)
    lane = lax.broadcasted_iota(jnp.int32, (ROWS, LANES), 1)
    second = pltpu.roll(first, steps_dev, 1)
    third = pltpu.roll(first, 2 * steps_dev, 1)
    days = jnp.where(lane < steps_dev, first, jnp.where(lane < 2 * steps_dev, second, third))
    return days[:, :lanes]


def sums_kernel(
    owner_ref,
    days_ref,
    field_ref,
    out_ref,
    lhs_ref,
    staged,
    scratch,
    sems,
    *,
    cols,
    band,
    width,
    chunk,
    steps_dev,
    radices,
):
    own_index = lax.axis_index("span")
    cells = field_ref.shape[1]
    groups = out_ref.shape[0]
    copies = []
    for c in range(cells // chunk):
        part = pl.ds(c * chunk, chunk)
        copy = pltpu.make_async_copy(field_ref.at[:, part], staged.at[:, part], sems.at[c])
        copy.start()
        copies.append(copy)
    lhs_ref[...] = split_design(own_days(days_ref, own_index, steps_dev), steps_dev, cols)
    scratch[:, cells:] = jnp.zeros((ROWS, scratch.shape[1] - cells), jnp.float32)
    lhs = lhs_ref[:, : 3 * steps_dev]
    placed = 0
    for c, copy in enumerate(copies):
        copy.wait()
        f = staged[:, c * chunk : (c + 1) * chunk]
        high = f.astype(jnp.bfloat16)
        left = f - high.astype(jnp.float32)
        mid = left.astype(jnp.bfloat16)
        low = (left - mid.astype(jnp.float32)).astype(jnp.bfloat16)
        stacked = jnp.concatenate([high, mid, low], 0)
        parts = jnp.dot(lhs, stacked, preferred_element_type=jnp.float32)
        total = parts[:ROWS] + (parts[ROWS : 2 * ROWS] + parts[2 * ROWS :])
        squares = jnp.sum(f * f, axis=0, keepdims=True)
        row = lax.broadcasted_iota(jnp.int32, total.shape, 0)
        scratch[:, c * chunk : (c + 1) * chunk] = jnp.where(row == cols, squares, total)
        while placed < groups and (placed + 1) * band <= (c + 1) * chunk:
            start = placed * band
            offset = start % LANES
            base = start - offset
            if offset:
                span = width + LANES
                block = pltpu.roll(scratch[:, base : base + span], span - offset, 1)[:, :width]
            else:
                block = scratch[:, base : base + width]
            target, source = owner_ref[placed], own_index
            place, inner = 0, groups
            for radix in radices:
                digit = lax.rem(lax.rem(target, radix) - lax.rem(source, radix) + radix, radix)
                target, source = lax.div(target, radix), lax.div(source, radix)
                inner //= radix
                place = place + digit * inner
            out_ref[place] = block
            placed += 1


def on_device(field, day_table, band_owner, sea_mask):
    groups = lax.axis_size("span")
    own_index = lax.axis_index("span")
    steps_dev, cells = field.shape
    band = cells // groups
    width = round_up(band, LANES)
    steps = day_table.shape[0]
    radices = split_radices(groups)
    strides = [math.prod(radices[:r]) for r in range(len(radices))]

    cols = 2 * HARMS + 1
    chunk = chunk_of(cells, 4608)
    lanes = round_up(3 * steps_dev, LANES)
    sums = pl.pallas_call(
        functools.partial(
            sums_kernel,
            cols=cols,
            band=band,
            width=width,
            chunk=chunk,
            steps_dev=steps_dev,
            radices=radices,
        ),
        in_specs=[
            pl.BlockSpec(memory_space=pltpu.SMEM),
            pl.BlockSpec(memory_space=pltpu.VMEM),
            pl.BlockSpec(memory_space=pl.ANY),
        ],
        out_specs=pl.BlockSpec(memory_space=pltpu.VMEM),
        out_shape=pltpu.VMEM((groups, ROWS, width), jnp.float32),
        scratch_shapes=[
            pltpu.VMEM((3 * ROWS, lanes), jnp.bfloat16),
            pltpu.VMEM((steps_dev, cells), jnp.float32),
            pltpu.VMEM((ROWS, cells + 2 * LANES), jnp.float32),
            pltpu.SemaphoreType.DMA((cells // chunk,)),
        ],
        name="sums",
    )(band_owner, day_table[None, :], field)

    slots = jnp.arange(groups, dtype=jnp.int32)
    lead = groups // radices[0]
    pieces = [sums[k * lead : (k + 1) * lead] for k in range(radices[0])]
    for r, (radix, stride) in enumerate(zip(radices, strides)):
        received = []
        for shift in range(1, radix):
            pairs = []
            for source in range(groups):
                digit = source // stride % radix
                pairs.append((source, source + ((digit + shift) % radix - digit) * stride))
            received.append(lax.ppermute(pieces[shift], "span", pairs))
        pieces = [pieces[0]] + received
        total = functools.reduce(jnp.add, pieces)
        if r == 0:
            late_days, total = lax.optimization_barrier((day_table, total))
        if r + 1 < len(radices):
            part = total.shape[0] // radices[r + 1]
            pieces = [total[k * part : (k + 1) * part] for k in range(radices[r + 1])]

    design = basis_rows(late_days[None, :].astype(jnp.float32), cols)
    gram = jnp.dot(design, design.T, precision=lax.Precision.HIGHEST)
    factor = jnp.linalg.cholesky(gram)
    inverse = lax.linalg.triangular_solve(
        factor, jnp.eye(cols, dtype=jnp.float32), left_side=True, lower=True
    )
    own_band = jnp.sum(jnp.where(band_owner == own_index, slots, 0))
    mask = lax.dynamic_slice_in_dim(sea_mask, own_band * band, band).astype(jnp.float32)
    mask = lax.optimization_barrier(mask)

    total = total[0, :, :band]
    half = jnp.dot(inverse, total[:cols], precision=lax.Precision.HIGHEST)
    coeffs = jnp.dot(inverse.T, half, precision=lax.Precision.HIGHEST)
    rest = total[cols] - jnp.sum(half * half, axis=0)
    variance = jnp.maximum(rest, 0.0) / steps
    return (coeffs * mask[None, :], variance * mask)


def solution(mesh):
    in_specs = (P(("member", "span"), None), P("member"), P("member"), P())
    out_specs = (P(None, ("member", "span")), P(("member", "span")))
    return jax.shard_map(
        on_device, mesh=mesh, in_specs=in_specs, out_specs=out_specs, check_vma=False
    )
```

time: 38.1 us -> 31.2 us (0.82)
  Pallas kernels: 8.66 us -> 3.64 us
  other arithmetic: 6.9 us -> 5.7 us
  waiting for transfers between devices: 7.16 us -> 6.21 us
    pallas_call x1, Pallas kernels: 8.66 us -> 3.64 us  [on_device(): pl.pallas_call(functools.partial(sums_kernel, cols=cols, band=band, width...]
    add x3, other arithmetic: 1.27 us -> 0.14 us  [on_device(): total = functools.reduce(jnp.add, pieces)]
    ppermute x7, waiting for transfers between devices: 7.16 us -> 6.21 us  [on_device(): received.append(lax.ppermute(pieces[shift], 'span', pairs))]
    convert_element_type x0 -> x2, other arithmetic: none -> 0.78 us  [the longest x1 0.78 us: on_device(): lax.dynamic_slice_in_dim(sea_mask, own_band * band, band)]
    mul x1, other arithmetic: 1.37 us -> 0.6 us  [on_device(): return (coeffs * mask[None, :], variance * mask)]
  transfers between devices with their start and end apart: 7 -> 7, of which waited for: 6 -> 5; matrix products, arithmetic and copies ran while one was open for 13% -> 18% of each run, Pallas kernels for 0% -> 0%
where the time goes in v3:
time: 31.2 us; the launch traced here: 30.9 us
  starting transfers between devices  12.1 us (39%)
  waiting for transfers between devices  6.21 us (20%)
  other arithmetic  5.7 us (18%)
  Pallas kernels  3.64 us (12%)
  matrix products  1.63 us (5%)
  between operations  1.4 us (4%)
    ppermute x7, starting transfers between devices, on_device(): received.append(lax.ppermute(pieces[shift], 'span', pairs))  12.1 us
    ppermute x7, waiting for transfers between devices, on_device(): received.append(lax.ppermute(pieces[shift], 'span', pairs))  6.21 us
    pallas_call x1, Pallas kernels, on_device(): pl.pallas_call(functools.partial(sums_kernel, cols=cols, band=band, width...  3.64 us
    another operation x3, other arithmetic, on_device(): factor = jnp.linalg.cholesky(gram)  1.87 us
    another operation x2, other arithmetic, on_device(): lax.linalg.triangular_solve(factor, jnp.eye(cols, dtype=jnp.float32), lef...  1.65 us
    dot_general x1, matrix products, on_device(): coeffs = jnp.dot(inverse.T, half, precision=lax.Precision.HIGHEST)  0.87 us
    convert_element_type x1, other arithmetic, on_device(): lax.dynamic_slice_in_dim(sea_mask, own_band * band, band)  0.78 us
    reduce_sum x1, other arithmetic, on_device(): own_band = jnp.sum(jnp.where(band_owner == own_index, slots, 0))  0.63 us
  transfers between devices with their start and end apart: 7, of which 5 were waited for; matrix products, arithmetic and copies ran while one was open for 18% of the time, Pallas kernels for 0%

profile of v3, /device:TPU:0, one launch (start us, length us, event | category | flops | bytes accessed | tf_op | source)
XLA Modules:
  0.0 30.9 jit_solution(6828120160469480100)
XLA Ops:
  0.6 3.6 %sums.1 = f32[32,16,768]{2,1,0:T(8,128)S(1)} custom-call(s32[32]{0:T(128)} %owner_ref.1, s32[1,1024]{1,0:T(1,128)} %bitcast.18, f32[32,23040]{1,0:T(8,128)} %field_ref.1), custom_call_target="tpu_custom_call" | custom-call | tf_op jit(solution)/shard_map/sums/pallas_call | solution.py:165
  4.3 0.0 copy-start.1
  4.3 0.1 slice.67
  4.3 0.6 %collective-permute-start = (f32[16,16,768]{2,1,0:T(8,128)S(1)}, f32[16,16,768]{2,1,0:T(8,128)S(1)}, u32[]{:S(2)}, u32[]{:S(2)}) collective-permute-start(f32[16,16,768]{2,1,0:T(8,128)S(1)} %slice.67), channel_id=1, source_target_pairs={{0,1},{1,0},{2,3},{3,2},{4,5},{5,4},{6,7},{7,6},{8,9},{9,8},{10,11... | collective-permute-start | bytes 2359304 | tf_op jit(solution)/shard_map/ppermute | solution.py:201
  4.9 0.0 copy-done.1
  4.9 0.6 %fusion.49 = s32[]{:T(128)} fusion(s32[32]{0:T(128)S(1)} %copy-done.1, s32[]{:T(128)S(6)} %axis_index.12), kind=kLoop, calls=%fused_computation.75 | loop fusion | flops 95 | bytes 136 | tf_op jit(solution)/shard_map/reduce_sum | solution.py:216
  6.2 0.8 %dynamic-slice_convert_fusion = f32[720]{0:T(1024)S(1)} fusion(s32[23040]{0:T(1024)} %param.7, s32[]{:T(128)S(6)} %select_n.46), kind=kLoop, calls=%fused_computation.66 | loop fusion | flops 720 | bytes 5764 | tf_op jit(solution)/shard_map/convert_element_type | solution.py:217
  7.0 0.0 copy-start
  7.0 0.0 collective-permute-done
  7.0 0.1 slice_add_fusion
  7.2 3.0 %collective-permute-start.1 = (f32[4,16,768]{2,1,0:T(8,128)S(1)}, f32[4,16,768]{2,1,0:T(8,128)S(1)}, u32[]{:S(2)}, u32[]{:S(2)}) collective-permute-start(f32[4,16,768]{2,1,0:T(8,128)S(1)} %get-tuple-element.6), channel_id=1, source_target_pairs={{0,2},{1,3},{2,4},{3,5},{4,6},{5,7},{6,0},{7,1},{8,10},{9,11},{10,... | collective-permute-start | bytes 589832 | tf_op jit(solution)/shard_map/ppermute | solution.py:201
  10.2 1.5 %collective-permute-start.2 = (f32[4,16,768]{2,1,0:T(8,128)S(1)}, f32[4,16,768]{2,1,0:T(8,128)S(1)}, u32[]{:S(2)}, u32[]{:S(2)}) collective-permute-start(f32[4,16,768]{2,1,0:T(8,128)S(1)} %get-tuple-element.8), channel_id=1, source_target_pairs={{0,4},{1,5},{2,6},{3,7},{4,0},{5,1},{6,2},{7,3},{8,12},{9,13},{10,... | collective-permute-start | bytes 589832 | tf_op jit(solution)/shard_map/ppermute | solution.py:201
  11.7 1.4 %collective-permute-start.3 = (f32[4,16,768]{2,1,0:T(8,128)S(1)}, f32[4,16,768]{2,1,0:T(8,128)S(1)}, u32[]{:S(2)}, u32[]{:S(2)}) collective-permute-start(f32[4,16,768]{2,1,0:T(8,128)S(1)} %get-tuple-element.7), channel_id=1, source_target_pairs={{0,6},{1,7},{2,0},{3,1},{4,2},{5,3},{6,4},{7,5},{8,14},{9,15},{10,... | collective-permute-start | bytes 589832 | tf_op jit(solution)/shard_map/ppermute | solution.py:201
  13.2 0.4 %fusion.2 = f32[13,13]{1,0:T(8,128)S(1)} fusion(s32[13]{0:T(128)S(1)} %get-tuple-element.17, s32[13]{0:T(128)S(1)} %get-tuple-element.18, f32[1024]{0:T(1024)S(1)} %convert_element_type.12, s32[13]{0:T(128)S(1)} %get-tuple-element.16, s32[13]{0:T(128)S(1)} %get-tuple-element.19, pred[13]{0:T(512)(128)(4,1)S(1)} %get-tuple-element.14, ...), kind=kOutput, calls=%fused_computation.6 | convolution fusion | flops 2569216 | bytes 5019 | tf_op jit(solution)/shard_map/dot_general | solution.py:211
  13.5 0.1 copy.6
  13.7 1.2 %cholesky.17 = f32[13,13]{1,0:T(8,128)S(1)} custom-call(f32[13,13]{1,0:T(8,128)S(1)} %fusion.48), custom_call_target="Cholesky" | custom-call | tf_op jit(solution)/shard_map/jit(cholesky)/cholesky | solution.py:212
  14.9 0.6 %compare_reduce_fusion = pred[]{:T(512)} fusion(f32[13]{0:T(128)S(1)} %select_reduce_fusion), kind=kLoop, calls=%fused_computation.69 | loop fusion | flops 25 | bytes 53 | tf_op jit(solution)/shard_map/jit(cholesky)/cholesky | solution.py:212
  15.6 0.6 %fusion.45 = f32[1,13,13]{2,1,0:T(8,128)S(1)} fusion(f32[13,13]{1,0:T(8,128)S(1)} %cholesky.17, pred[]{:T(512)} %compare_reduce_fusion), kind=kLoop, calls=%fused_computation.57 | loop fusion | flops 676 | bytes 1353 | tf_op jit(solution)/shard_map/triangular_solve | solution.py:213
  16.2 1.0 %custom-call.6 = f32[1,13,13]{1,2,0:T(8,128)S(1)} custom-call(f32[1,13,13]{2,1,0:T(8,128)S(1)} %fusion.45), custom_call_target="InvertDiagBlocksLowerTriangular" | custom-call | tf_op jit(solution)/shard_map/triangular_solve | solution.py:213
  17.2 0.0 collective-permute-done.1
  17.2 3.2 %collective-permute-done.2 = f32[4,16,768]{2,1,0:T(8,128)S(1)} collective-permute-done((f32[4,16,768]{2,1,0:T(8,128)S(1)}, f32[4,16,768]{2,1,0:T(8,128)S(1)}, u32[]{:S(2)}, u32[]{:S(2)}) %collective-permute-start.2) | collective-permute-done | bytes 196640 | tf_op jit(solution)/shard_map/ppermute | solution.py:201
  20.4 0.3 collective-permute-done.3
  20.8 1.6 %collective-permute-start.4 = (f32[1,16,768]{2,1,0:T(8,128)S(1)}, f32[1,16,768]{2,1,0:T(8,128)S(1)}, u32[]{:S(2)}, u32[]{:S(2)}) collective-permute-start(f32[1,16,768]{2,1,0:T(8,128)S(1)} %get-tuple-element.9), channel_id=1, source_target_pairs={{0,8},{1,9},{2,10},{3,11},{4,12},{5,13},{6,14},{7,15},{8,16},{9,17... | collective-permute-start | bytes 147464 | tf_op jit(solution)/shard_map/ppermute | solution.py:201
  22.4 2.6 %collective-permute-start.5 = (f32[1,16,768]{2,1,0:T(8,128)S(1)}, f32[1,16,768]{2,1,0:T(8,128)S(1)}, u32[]{:S(2)}, u32[]{:S(2)}) collective-permute-start(f32[1,16,768]{2,1,0:T(8,128)S(1)} %get-tuple-element.11), channel_id=1, source_target_pairs={{0,16},{1,17},{2,18},{3,19},{4,20},{5,21},{6,22},{7,23},{8,24},{9,... | collective-permute-start | bytes 147464 | tf_op jit(solution)/shard_map/ppermute | solution.py:201
  25.0 1.3 %collective-permute-start.6 = (f32[1,16,768]{2,1,0:T(8,128)S(1)}, f32[1,16,768]{2,1,0:T(8,128)S(1)}, u32[]{:S(2)}, u32[]{:S(2)}) collective-permute-start(f32[1,16,768]{2,1,0:T(8,128)S(1)} %get-tuple-element.10), channel_id=1, source_target_pairs={{0,24},{1,25},{2,26},{3,27},{4,28},{5,29},{6,30},{7,31},{8,0},{9,1... | collective-permute-start | bytes 147464 | tf_op jit(solution)/shard_map/ppermute | solution.py:201
  26.4 0.2 fusion.46
  26.6 0.4 %collective-permute-done.4 = f32[1,16,768]{2,1,0:T(8,128)S(1)} collective-permute-done((f32[1,16,768]{2,1,0:T(8,128)S(1)}, f32[1,16,768]{2,1,0:T(8,128)S(1)}, u32[]{:S(2)}, u32[]{:S(2)}) %collective-permute-start.4) | collective-permute-done | bytes 49184 | tf_op jit(solution)/shard_map/ppermute | solution.py:201
  26.9 1.9 %collective-permute-done.5 = f32[1,16,768]{2,1,0:T(8,128)S(1)} collective-permute-done((f32[1,16,768]{2,1,0:T(8,128)S(1)}, f32[1,16,768]{2,1,0:T(8,128)S(1)}, u32[]{:S(2)}, u32[]{:S(2)}) %collective-permute-start.5) | collective-permute-done | bytes 49184 | tf_op jit(solution)/shard_map/ppermute | solution.py:201
  28.8 0.4 %collective-permute-done.6 = f32[1,16,768]{2,1,0:T(8,128)S(1)} collective-permute-done((f32[1,16,768]{2,1,0:T(8,128)S(1)}, f32[1,16,768]{2,1,0:T(8,128)S(1)}, u32[]{:S(2)}, u32[]{:S(2)}) %collective-permute-start.6) | collective-permute-done | bytes 49184 | tf_op jit(solution)/shard_map/ppermute | solution.py:201
  29.3 0.2 multiply_reduce_fusion
  29.5 0.9 %convolution_multiply_fusion = f32[13,720]{1,0:T(8,128)} fusion(f32[13,13]{1,0:T(8,128)S(1)} %fusion.46, f32[13,720]{1,0:T(8,128)S(1)} %get-tuple-element.13, f32[720]{0:T(1024)S(1)} %dynamic-slice_convert_fusion), kind=kOutput, calls=%fused_computation | convolution fusion | flops 1469520 | bytes 78436 | tf_op jit(solution)/shard_map/dot_general | solution.py:222
  30.3 0.6 %multiply_multiply_fusion.4 = f32[720]{0:T(1024)} fusion(f32[720]{0:T(1024)S(1)} %dynamic-slice_convert_fusion, f32[720]{0:T(1024)S(1)} %slice_reduce_fusion, f32[720]{0:T(1024)S(1)} %get-tuple-element.12), kind=kLoop, calls=%fused_computation.65 | loop fusion | flops 2880 | bytes 11520 | tf_op jit(solution)/shard_map/mul | solution.py:225
  (13 shorter events, 0.2 us)
Async XLA Ops:
  4.3 0.7 %copy-start.1 = (s32[32]{0:T(128)S(1)}, s32[32]{0:T(128)}, u32[]{:S(2)}) copy-start(s32[32]{0:T(128)} %owner_ref.1) | copy-start | bytes 388
  4.3 2.7 %collective-permute-start = (f32[16,16,768]{2,1,0:T(8,128)S(1)}, f32[16,16,768]{2,1,0:T(8,128)S(1)}, u32[]{:S(2)}, u32[]{:S(2)}) collective-permute-start(f32[16,16,768]{2,1,0:T(8,128)S(1)} %slice.67), channel_id=1, source_target_pairs={{0,1},{1,0},{2,3},{3,2},{4,5},{5,4},{6,7},{7,6},{8,9},{9,8},{10,11... | collective-permute-start | bytes 2359304 | tf_op jit(solution)/shard_map/ppermute | solution.py:201
  7.0 6.1 %copy-start = (s32[1024]{0:T(1024)S(1)}, s32[1024]{0:T(1024)}, u32[]{:S(2)}) copy-start(s32[1024]{0:T(1024)} %param.5) | copy-start | bytes 12292
  7.2 10.0 %collective-permute-start.1 = (f32[4,16,768]{2,1,0:T(8,128)S(1)}, f32[4,16,768]{2,1,0:T(8,128)S(1)}, u32[]{:S(2)}, u32[]{:S(2)}) collective-permute-start(f32[4,16,768]{2,1,0:T(8,128)S(1)} %get-tuple-element.6), channel_id=1, source_target_pairs={{0,2},{1,3},{2,4},{3,5},{4,6},{5,7},{6,0},{7,1},{8,10},{9,11},{10,... | collective-permute-start | bytes 589832 | tf_op jit(solution)/shard_map/ppermute | solution.py:201
  10.2 10.2 %collective-permute-start.2 = (f32[4,16,768]{2,1,0:T(8,128)S(1)}, f32[4,16,768]{2,1,0:T(8,128)S(1)}, u32[]{:S(2)}, u32[]{:S(2)}) collective-permute-start(f32[4,16,768]{2,1,0:T(8,128)S(1)} %get-tuple-element.8), channel_id=1, source_target_pairs={{0,4},{1,5},{2,6},{3,7},{4,0},{5,1},{6,2},{7,3},{8,12},{9,13},{10,... | collective-permute-start | bytes 589832 | tf_op jit(solution)/shard_map/ppermute | solution.py:201
  11.7 9.0 %collective-permute-start.3 = (f32[4,16,768]{2,1,0:T(8,128)S(1)}, f32[4,16,768]{2,1,0:T(8,128)S(1)}, u32[]{:S(2)}, u32[]{:S(2)}) collective-permute-start(f32[4,16,768]{2,1,0:T(8,128)S(1)} %get-tuple-element.7), channel_id=1, source_target_pairs={{0,6},{1,7},{2,0},{3,1},{4,2},{5,3},{6,4},{7,5},{8,14},{9,15},{10,... | collective-permute-start | bytes 589832 | tf_op jit(solution)/shard_map/ppermute | solution.py:201
  20.8 6.1 %collective-permute-start.4 = (f32[1,16,768]{2,1,0:T(8,128)S(1)}, f32[1,16,768]{2,1,0:T(8,128)S(1)}, u32[]{:S(2)}, u32[]{:S(2)}) collective-permute-start(f32[1,16,768]{2,1,0:T(8,128)S(1)} %get-tuple-element.9), channel_id=1, source_target_pairs={{0,8},{1,9},{2,10},{3,11},{4,12},{5,13},{6,14},{7,15},{8,16},{9,17... | collective-permute-start | bytes 147464 | tf_op jit(solution)/shard_map/ppermute | solution.py:201
  22.4 6.4 %collective-permute-start.5 = (f32[1,16,768]{2,1,0:T(8,128)S(1)}, f32[1,16,768]{2,1,0:T(8,128)S(1)}, u32[]{:S(2)}, u32[]{:S(2)}) collective-permute-start(f32[1,16,768]{2,1,0:T(8,128)S(1)} %get-tuple-element.11), channel_id=1, source_target_pairs={{0,16},{1,17},{2,18},{3,19},{4,20},{5,21},{6,22},{7,23},{8,24},{9,... | collective-permute-start | bytes 147464 | tf_op jit(solution)/shard_map/ppermute | solution.py:201
  25.0 4.2 %collective-permute-start.6 = (f32[1,16,768]{2,1,0:T(8,128)S(1)}, f32[1,16,768]{2,1,0:T(8,128)S(1)}, u32[]{:S(2)}, u32[]{:S(2)}) collective-permute-start(f32[1,16,768]{2,1,0:T(8,128)S(1)} %get-tuple-element.10), channel_id=1, source_target_pairs={{0,24},{1,25},{2,26},{3,27},{4,28},{5,29},{6,30},{7,31},{8,0},{9,1... | collective-permute-start | bytes 147464 | tf_op jit(solution)/shard_map/ppermute | solution.py:201
